TPU v7x, 256 devices: a whole 4x4x8 slice. The times are simulated.
256 devices in a mesh: batch: 4 (over x), proto: 64 (over y, z, core).
Axes of the slice: x: 4, y: 4, z: 8, core: 2. Of those that a mesh axis runs over, the one named last changes fastest.
Arguments:
- view_codes: bfloat16 [4096, 1024], P('batch', 'proto'), may hold values from -80 to 80
- predictor_view_embeddings: bfloat16 [4096, 1024], P('batch', 'proto'), may hold values from -80 to 80
- prototypes: bfloat16 [65536, 1024], P('proto'), may hold values from -64 to 64
Outputs:
- assignments: bfloat16 [4096, 65536], P('batch', 'proto')
- loss_rows: float32 [4096], P('batch')
All inputs are finite; a program needn't handle non-finite values.
Results may differ from a plain program's by a relative error of at most 0.0034.
Values may be sent and summed in bfloat16 or wider, within the bound.
A program may use at most 64 MiB of HBM per device.

v0:
```python
import jax
import jax.numpy as jnp
from jax import lax
from jax.sharding import PartitionSpec as P

SINK_ITERS = 3
EPSILON = 0.05
SOFTMAX_TEMP_VALUE = 0.1


def copy_for_each(shard, axis):
    copies = jnp.broadcast_to(shard, (lax.axis_size(axis), *shard.shape))
    return lax.all_to_all(copies, axis, split_axis=0, concat_axis=0, tiled=True)


def of_everyone(shard, axis):
    return copy_for_each(shard, axis).sum(axis=0)


def together(arrays, axis):
    ravelled, at, gathered = (jnp.concatenate([a.reshape(-1) for a in arrays]), 0, [])
    subtotal = of_everyone(ravelled, axis)
    for a in arrays:
        gathered.append(subtotal[at : at + a.size].reshape(a.shape))
        at += a.size
    return tuple(gathered)


def normalized(prototypes):
    weights = prototypes.astype(jnp.float32)
    return (weights * lax.rsqrt(jnp.sum(weights * weights, axis=1, keepdims=True) + 1e-06)).astype(
        jnp.bfloat16
    )


def view_scores(embedded, unit_prototype_rows):
    products = jnp.dot(embedded, unit_prototype_rows.T, preferred_element_type=jnp.float32)
    values = embedded.astype(jnp.float32)
    inverse_factor = lax.rsqrt(jnp.sum(values * values, axis=1) + 1e-06)
    return products * inverse_factor[:, None]


def local(view_codes, predictor_view_embeddings, prototypes):
    unit_prototype_rows = normalized(prototypes)
    whole_first, whole_second = (
        lax.all_gather(view_codes, "proto", axis=1, tiled=True),
        lax.all_gather(predictor_view_embeddings, "proto", axis=1, tiled=True),
    )
    scores_codes = view_scores(whole_first, unit_prototype_rows)
    predictor_scores = view_scores(whole_second, unit_prototype_rows)
    kernel = jnp.exp(scores_codes / EPSILON)
    rows_total = kernel.shape[0] * lax.axis_size("batch")
    protos_total = kernel.shape[1] * lax.axis_size("proto")
    logit_scores = predictor_scores / SOFTMAX_TEMP_VALUE
    scale_rows = jnp.ones((kernel.shape[0],), jnp.float32)
    for iteration in range(SINK_ITERS):
        col_part = jnp.dot(scale_rows, kernel, precision=lax.Precision.HIGHEST)
        col_sums = of_everyone(col_part, "batch")
        scale_cols = 1.0 / (protos_total * col_sums)
        row_part = jnp.dot(kernel, scale_cols, precision=lax.Precision.HIGHEST)
        row_sums = of_everyone(row_part, "proto")
        scale_rows = 1.0 / (rows_total * row_sums)
    assign = kernel * scale_cols[None, :] * (rows_total * scale_rows)[:, None]
    assignments = (protos_total * assign).astype(jnp.bfloat16)
    cross_part = jnp.sum(assign * logit_scores, axis=1)
    totals, cross_term = together((jnp.sum(jnp.exp(logit_scores), axis=1), cross_part), "proto")
    loss_rows = jnp.log(totals) - cross_term
    return (assignments, loss_rows)


def solution(mesh):
    placed = (P("batch", "proto"), P("batch", "proto"), P("proto", None))
    return jax.shard_map(
        local,
        mesh=mesh,
        in_specs=placed,
        out_specs=(P("batch", "proto"), P("batch")),
        check_vma=False,
    )
```

profile of v0, /device:TPU:1, one launch (start us, length us, event | category | flops | bytes accessed | tf_op | source)
XLA Modules:
  0.0 249.5 jit_solution(1705991306893637967)
XLA Ops:
  8.7 2.1 fusion
  10.7 81.8 %all-gather.3.cloned.1.call-done = bf16[1024,1024]{0,1:T(8,128)(2,1)} async-done(((bf16[1024,16]{0,1:T(8,128)(2,1)}), bf16[1024,1024]{0,1:T(8,128)(2,1)}) %all-gather.3.cloned.1.call-update) | async-done | bytes 2097168 | tf_op jit(solution)/shard_map/all_gather | solution.py:46
  92.6 2.1 multiply_reduce_fusion.1
  94.7 4.0 %multiply_exponential_fusion = f32[1024,1024]{1,0:T(8,128)S(1)} fusion(bf16[1024,1024]{0,1:T(8,128)(2,1)} %all-gather.3.cloned.1.call-done, f32[1024]{0:T(1024)S(1)} %add_rsqrt_fusion.1, bf16[1024,1024]{1,0:T(8,128)(2,1)S(1)} %copy-done.1, f32[1024]{0:T(1024)S(1)} %add_rsqrt_fusion.2), kind=kOutput, calls=%fused_computation.25 | convolution fusion | flops 2152726528 | bytes 8396800 | tf_op jit(solution)/shard_map/dot_general | solution.py:37
  98.7 1.9 copy-done
  100.6 3.6 %fusion.14 = f32[1,1024]{1,0:T(1,128)S(1)} fusion(f32[1024,1024]{1,0:T(8,128)S(1)} %multiply_exponential_fusion), kind=kOutput, calls=%fused_computation.19 | convolution fusion | flops 12582912 | bytes 4198400 | tf_op jit(solution)/shard_map/dot_general | solution.py:57
  104.2 8.1 %all_to_all.42 = f32[4,1,1024]{2,1,0:T(1,128)S(1)} all-to-all(f32[4,1,1024]{2,1,0:T(1,128)S(1)} %broadcast_in_dim.26), channel_id=1, replica_groups=mesh['batch'=4,'proto'=64] {'batch'}, dimensions={0} | all-to-all | bytes 32768 | tf_op jit(solution)/shard_map/all_to_all | solution.py:13
  112.2 4.4 %fusion.12 = f32[1,1024]{1,0:T(1,128)S(1)} fusion(f32[1024,1]{0,1:T(1,128)S(1)} %bitcast.52, f32[1024,1024]{1,0:T(8,128)} %copy-done), kind=kOutput, calls=%fused_computation.17 | convolution fusion | flops 12582912 | bytes 4202496 | tf_op jit(solution)/shard_map/dot_general | solution.py:60
  116.8 19.7 %all_to_all.43 = f32[64,1,1024]{2,1,0:T(1,128)S(1)} all-to-all(f32[64,1,1024]{2,1,0:T(1,128)S(1)} %broadcast_in_dim.27), channel_id=1, replica_groups=mesh['batch'=4,'proto'=64] {'proto'}, dimensions={0} | all-to-all | bytes 524288 | tf_op jit(solution)/shard_map/all_to_all | solution.py:13
  136.7 5.6 %fusion.10 = f32[1,1024]{1,0:T(1,128)S(1)} fusion(f32[1024,1]{0,1:T(1,128)S(1)} %bitcast.53, f32[1024,1024]{1,0:T(8,128)} %copy-done), kind=kOutput, calls=%fused_computation.15 | convolution fusion | flops 12582912 | bytes 4202496 | tf_op jit(solution)/shard_map/dot_general | solution.py:57
  142.4 6.6 %all_to_all.44 = f32[4,1,1024]{2,1,0:T(1,128)S(1)} all-to-all(f32[4,1,1024]{2,1,0:T(1,128)S(1)} %broadcast_in_dim.28), channel_id=1, replica_groups=mesh['batch'=4,'proto'=64] {'batch'}, dimensions={0} | all-to-all | bytes 32768 | tf_op jit(solution)/shard_map/all_to_all | solution.py:13
  149.0 4.4 %fusion.8 = f32[1,1024]{1,0:T(1,128)S(1)} fusion(f32[1024,1]{0,1:T(1,128)S(1)} %bitcast.54, f32[1024,1024]{1,0:T(8,128)} %copy-done), kind=kOutput, calls=%fused_computation.13 | convolution fusion | flops 12582912 | bytes 4202496 | tf_op jit(solution)/shard_map/dot_general | solution.py:60
  153.6 19.1 %all_to_all.45 = f32[64,1,1024]{2,1,0:T(1,128)S(1)} all-to-all(f32[64,1,1024]{2,1,0:T(1,128)S(1)} %broadcast_in_dim.29), channel_id=1, replica_groups=mesh['batch'=4,'proto'=64] {'proto'}, dimensions={0} | all-to-all | bytes 524288 | tf_op jit(solution)/shard_map/all_to_all | solution.py:13
  172.8 5.6 %fusion.6 = f32[1,1024]{1,0:T(1,128)S(1)} fusion(f32[1024,1]{0,1:T(1,128)S(1)} %bitcast.55, f32[1024,1024]{1,0:T(8,128)} %copy-done), kind=kOutput, calls=%fused_computation.11 | convolution fusion | flops 12582912 | bytes 4202496 | tf_op jit(solution)/shard_map/dot_general | solution.py:57
  178.5 6.6 %all_to_all.46 = f32[4,1,1024]{2,1,0:T(1,128)S(1)} all-to-all(f32[4,1,1024]{2,1,0:T(1,128)S(1)} %broadcast_in_dim.30), channel_id=1, replica_groups=mesh['batch'=4,'proto'=64] {'batch'}, dimensions={0} | all-to-all | bytes 32768 | tf_op jit(solution)/shard_map/all_to_all | solution.py:13
  185.1 4.4 %fusion.4 = f32[1,1024]{1,0:T(1,128)S(1)} fusion(f32[1024,1]{0,1:T(1,128)S(1)} %bitcast.51, f32[1024,1024]{1,0:T(8,128)} %copy-done), kind=kOutput, calls=%fused_computation.8 | convolution fusion | flops 12582912 | bytes 4202496 | tf_op jit(solution)/shard_map/dot_general | solution.py:60
  190.4 7.9 %all-to-all-start.5 = ((f32[64,1,1024]{2,1,0:T(1,128)}), f32[64,1,1024]{2,1,0:T(1,128)S(1)}, u32[]{:S(2)}, u32[]{:S(2)}) async-start(f32[64,1,1024]{2,1,0:T(1,128)} %broadcast_in_dim.31), calls=%async_computation.5 | async-start | bytes 524288 | tf_op jit(solution)/shard_map/all_to_all | solution.py:13
  198.3 2.1 multiply_reduce_fusion
  200.4 9.9 %all-to-all-done.5 = f32[64,1,1024]{2,1,0:T(1,128)S(1)} async-done(((f32[64,1,1024]{2,1,0:T(1,128)}), f32[64,1,1024]{2,1,0:T(1,128)S(1)}, u32[]{:S(2)}, u32[]{:S(2)}) %all-to-all-start.5) | async-done | bytes 262176 | tf_op jit(solution)/shard_map/all_to_all | solution.py:13
  210.5 6.9 %fusion.2 = (f32[1024]{0:T(1024)S(1)}, f32[1024]{0:T(1024)S(1)}, bf16[1024,1024]{0,1:T(8,128)(2,1)}) fusion(f32[1024]{0:T(1024)S(1)} %add_rsqrt_fusion, f32[1024]{0:T(1024)S(1)} %divide_multiply_fusion, f32[1024]{0:T(1024)S(1)} %multiply_divide_fusion, f32[1024,1024]{1,0:T(8,128)} %copy-done, bf16[1024,1024]{0,1:T(8,128)(2,1)} %all-gather.5.cloned.1.call-done, ...), kind=kOutput, calls=%fused_computation.6 | convolution fusion | flops 2160064512 | bytes 10510336 | tf_op jit(solution)/shard_map/dot_general | solution.py:37
  217.3 1.1 broadcast_in_dim.32
  218.4 6.0 %all-to-all-start.6 = ((f32[64,1,2048]{2,1,0:T(1,128)}), f32[64,1,2048]{2,1,0:T(1,128)S(1)}, u32[]{:S(2)}, u32[]{:S(2)}) async-start(f32[64,1,2048]{2,1,0:T(1,128)} %broadcast_in_dim.32), calls=%async_computation.6 | async-start | bytes 1048576 | tf_op jit(solution)/shard_map/all_to_all | solution.py:13
  224.4 3.9 %copy.14 = bf16[1024,1024]{1,0:T(8,128)(2,1)} copy(bf16[1024,1024]{0,1:T(8,128)(2,1)} %get-tuple-element.10) | data formatting | bytes 4194304
  228.4 13.3 %all-to-all-done.6 = f32[64,1,2048]{2,1,0:T(1,128)S(1)} async-done(((f32[64,1,2048]{2,1,0:T(1,128)}), f32[64,1,2048]{2,1,0:T(1,128)S(1)}, u32[]{:S(2)}, u32[]{:S(2)}) %all-to-all-start.6) | async-done | bytes 524320 | tf_op jit(solution)/shard_map/all_to_all | solution.py:13
  (32 shorter events, 4.3 us)
Async XLA Ops:
  7.2 87.5 %copy-start.1 = (bf16[1024,1024]{1,0:T(8,128)(2,1)S(1)}, bf16[1024,1024]{1,0:T(8,128)(2,1)}, u32[]{:S(2)}) copy-start(bf16[1024,1024]{1,0:T(8,128)(2,1)} %param.5) | copy-start | bytes 6291460
  7.2 85.4 %all-gather.3.cloned.1.call-start = ((), (), s32[]{:S(2)}) async-start(), calls=%async_computation.7 | async-start | bytes 2129920 | tf_op jit(solution)/shard_map/all_gather | solution.py:46
  7.9 190.4 %all-gather.5.cloned.1.call-start = ((), (), s32[]{:S(2)}) async-start(), calls=%async_computation.8 | async-start | bytes 2129920 | tf_op jit(solution)/shard_map/all_gather | solution.py:47
  98.6 1.9 copy-start
  190.4 19.9 %all-to-all-start.5 = ((f32[64,1,1024]{2,1,0:T(1,128)}), f32[64,1,1024]{2,1,0:T(1,128)S(1)}, u32[]{:S(2)}, u32[]{:S(2)}) async-start(f32[64,1,1024]{2,1,0:T(1,128)} %broadcast_in_dim.31), calls=%async_computation.5 | async-start | bytes 524288 | tf_op jit(solution)/shard_map/all_to_all | solution.py:13
  218.4 23.3 %all-to-all-start.6 = ((f32[64,1,2048]{2,1,0:T(1,128)}), f32[64,1,2048]{2,1,0:T(1,128)S(1)}, u32[]{:S(2)}, u32[]{:S(2)}) async-start(f32[64,1,2048]{2,1,0:T(1,128)} %broadcast_in_dim.32), calls=%async_computation.6 | async-start | bytes 1048576 | tf_op jit(solution)/shard_map/all_to_all | solution.py:13
Sparse Core Ops, SparseCore 0:
  10.8 81.7 all-gather.2
  95.3 75.9 all-gather.4
where the time goes:
time: 250 us; the launch traced here: 249 us
  waiting for transfers between devices  106 us (42%)
  blocking collectives  59.9 us (24%)
  matrix products  39 us (16%)
  between operations  14.2 us (6%)
  starting transfers between devices  14 us (6%)
  local copies, waits for them, and re-layouts  8.12 us (3%)
  other arithmetic  7.8 us (3%)
    all_gather x1, waiting for transfers between devices, local(): lax.all_gather(view_codes, 'proto', axis=1, tiled=True)  81.8 us
    all_to_all x5, blocking collectives, copy_for_each(): return lax.all_to_all(copies, axis, split_axis=0, concat_axis=0, tiled=True)  59.9 us
    all_to_all x2, waiting for transfers between devices, copy_for_each(): return lax.all_to_all(copies, axis, split_axis=0, concat_axis=0, tiled=True)  23.2 us
    dot_general x3, matrix products, local(): col_part = jnp.dot(scale_rows, kernel, precision=lax.Precision.HIGHEST)  14.9 us
    all_to_all x2, starting transfers between devices, copy_for_each(): return lax.all_to_all(copies, axis, split_axis=0, concat_axis=0, tiled=True)  13.9 us
    dot_general x3, matrix products, local(): row_part = jnp.dot(kernel, scale_cols, precision=lax.Precision.HIGHEST)  13.3 us
    dot_general x2, matrix products, view_scores(): jnp.dot(embedded, unit_prototype_rows.T, preferred_element_type=jnp.float32)  10.9 us
    unnamed x5, local copies, waits for them, and re-layouts  5.86 us
  transfers between devices with their start and end apart: 4, of which 3 were waited for; matrix products, arithmetic and copies ran while one was open for 18% of the time, Pallas kernels for 0%

commit v1 on v0

--- a/solution.py
+++ b/solution.py
@@ -43,7 +43,9 @@
 def local(view_codes, predictor_view_embeddings, prototypes):
     unit_prototype_rows = normalized(prototypes)
     whole_first, whole_second = (
-        lax.all_gather(view_codes, "proto", axis=1, tiled=True),
+        jnp.concatenate(
+            lax.all_to_all(jnp.stack([view_codes] * lax.axis_size("proto")), "proto", 0, 0), axis=1
+        ),
         lax.all_gather(predictor_view_embeddings, "proto", axis=1, tiled=True),
     )
     scores_codes = view_scores(whole_first, unit_prototype_rows)

time: 250 us -> 230 us (0.920)
  waiting for transfers between devices: 106 us -> 73.5 us
  starting transfers between devices: 14 us -> 26.6 us
    all_gather x1 -> x0, waiting for transfers between devices: 81.8 us -> none  [local(): lax.all_gather(view_codes, 'proto', axis=1, tiled=True)]
    all_to_all x0 -> x1, waiting for transfers between devices: none -> 49.6 us  [local(): lax.all_to_all(jnp.stack([view_codes] * lax.axis_size('proto')), 'proto',...]
    all_to_all x0 -> x1, starting transfers between devices: none -> 13.1 us  [local(): lax.all_to_all(jnp.stack([view_codes] * lax.axis_size('proto')), 'proto',...]
where the time goes in v1:
time: 230 us; the launch traced here: 229 us
  waiting for transfers between devices  73.5 us (32%)
  blocking collectives  59.3 us (26%)
  matrix products  39 us (17%)
  starting transfers between devices  26.6 us (12%)
  between operations  14.2 us (6%)
  local copies, waits for them, and re-layouts  10.5 us (5%)
  other arithmetic  6.21 us (3%)
    all_to_all x5, blocking collectives, copy_for_each(): return lax.all_to_all(copies, axis, split_axis=0, concat_axis=0, tiled=True)  59.3 us
    all_to_all x1, waiting for transfers between devices, local(): lax.all_to_all(jnp.stack([view_codes] * lax.axis_size('proto')), 'proto',...  49.6 us
    all_to_all x2, waiting for transfers between devices, copy_for_each(): return lax.all_to_all(copies, axis, split_axis=0, concat_axis=0, tiled=True)  23.2 us
    dot_general x3, matrix products, local(): col_part = jnp.dot(scale_rows, kernel, precision=lax.Precision.HIGHEST)  14.9 us
    all_to_all x2, starting transfers between devices, copy_for_each(): return lax.all_to_all(copies, axis, split_axis=0, concat_axis=0, tiled=True)  13.4 us
    dot_general x3, matrix products, local(): row_part = jnp.dot(kernel, scale_cols, precision=lax.Precision.HIGHEST)  13.3 us
    all_to_all x1, starting transfers between devices, local(): lax.all_to_all(jnp.stack([view_codes] * lax.axis_size('proto')), 'proto',...  13.1 us
    dot_general x2, matrix products, view_scores(): jnp.dot(embedded, unit_prototype_rows.T, preferred_element_type=jnp.float32)  10.9 us
  transfers between devices with their start and end apart: 4, of which 3 were waited for; matrix products, arithmetic and copies ran while one was open for 18% of the time, Pallas kernels for 0%

profile of v1, /device:TPU:1, one launch (start us, length us, event | category | flops | bytes accessed | tf_op | source)
XLA Modules:
  0.0 229.3 jit_solution(16280516851337928532)
XLA Ops:
  7.2 2.3 %stack.2 = bf16[64,1024,16]{1,2,0:T(8,128)(2,1)} broadcast(bf16[1024,16]{0,1:T(8,128)(2,1)} %param.3), dimensions={1,2} | broadcast | bytes 2129920 | tf_op jit(solution)/shard_map/stack | solution.py:47
  9.5 13.1 %all-to-all-start = ((bf16[64,1024,16]{1,2,0:T(8,128)(2,1)}), bf16[64,1024,16]{1,2,0:T(8,128)(2,1)S(1)}, u32[]{:S(2)}, u32[]{:S(2)}) async-start(bf16[64,1024,16]{1,2,0:T(8,128)(2,1)} %stack.2), calls=%async_computation | async-start | bytes 4194304 | tf_op jit(solution)/shard_map/all_to_all | solution.py:47
  23.4 2.1 fusion
  25.5 49.6 %all-to-all-done = bf16[64,1024,16]{1,2,0:T(8,128)(2,1)S(1)} async-done(((bf16[64,1024,16]{1,2,0:T(8,128)(2,1)}), bf16[64,1024,16]{1,2,0:T(8,128)(2,1)S(1)}, u32[]{:S(2)}, u32[]{:S(2)}) %all-to-all-start) | async-done | bytes 2097184 | tf_op jit(solution)/shard_map/all_to_all | solution.py:47
  75.5 4.0 %multiply_exponential_fusion = f32[1024,1024]{1,0:T(8,128)S(1)} fusion(bf16[1024,1024]{0,1:T(8,128)(2,1)S(1)} %bitcast.49, f32[1024]{0:T(1024)S(1)} %add_rsqrt_fusion.1, bf16[1024,1024]{1,0:T(8,128)(2,1)} %param.5, f32[1024]{0:T(1024)S(1)} %add_rsqrt_fusion.2), kind=kOutput, calls=%fused_computation.25 | convolution fusion | flops 2152726528 | bytes 8396800 | tf_op jit(solution)/shard_map/dot_general | solution.py:37
  79.5 1.9 copy-done
  81.5 3.6 %fusion.14 = f32[1,1024]{1,0:T(1,128)S(1)} fusion(f32[1024,1024]{1,0:T(8,128)S(1)} %multiply_exponential_fusion), kind=kOutput, calls=%fused_computation.19 | convolution fusion | flops 12582912 | bytes 4198400 | tf_op jit(solution)/shard_map/dot_general | solution.py:59
  85.0 8.0 %all_to_all.47 = f32[4,1,1024]{2,1,0:T(1,128)S(1)} all-to-all(f32[4,1,1024]{2,1,0:T(1,128)S(1)} %broadcast_in_dim.26), channel_id=1, replica_groups=mesh['batch'=4,'proto'=64] {'batch'}, dimensions={0} | all-to-all | bytes 32768 | tf_op jit(solution)/shard_map/all_to_all | solution.py:13
  93.1 4.4 %fusion.12 = f32[1,1024]{1,0:T(1,128)S(1)} fusion(f32[1024,1]{0,1:T(1,128)S(1)} %bitcast.57, f32[1024,1024]{1,0:T(8,128)} %copy-done), kind=kOutput, calls=%fused_computation.17 | convolution fusion | flops 12582912 | bytes 4202496 | tf_op jit(solution)/shard_map/dot_general | solution.py:62
  97.7 19.1 %all_to_all.48 = f32[64,1,1024]{2,1,0:T(1,128)S(1)} all-to-all(f32[64,1,1024]{2,1,0:T(1,128)S(1)} %broadcast_in_dim.27), channel_id=1, replica_groups=mesh['batch'=4,'proto'=64] {'proto'}, dimensions={0} | all-to-all | bytes 524288 | tf_op jit(solution)/shard_map/all_to_all | solution.py:13
  116.9 5.6 %fusion.10 = f32[1,1024]{1,0:T(1,128)S(1)} fusion(f32[1024,1]{0,1:T(1,128)S(1)} %bitcast.58, f32[1024,1024]{1,0:T(8,128)} %copy-done), kind=kOutput, calls=%fused_computation.15 | convolution fusion | flops 12582912 | bytes 4202496 | tf_op jit(solution)/shard_map/dot_general | solution.py:59
  122.6 6.6 %all_to_all.49 = f32[4,1,1024]{2,1,0:T(1,128)S(1)} all-to-all(f32[4,1,1024]{2,1,0:T(1,128)S(1)} %broadcast_in_dim.28), channel_id=1, replica_groups=mesh['batch'=4,'proto'=64] {'batch'}, dimensions={0} | all-to-all | bytes 32768 | tf_op jit(solution)/shard_map/all_to_all | solution.py:13
  129.2 4.4 %fusion.8 = f32[1,1024]{1,0:T(1,128)S(1)} fusion(f32[1024,1]{0,1:T(1,128)S(1)} %bitcast.59, f32[1024,1024]{1,0:T(8,128)} %copy-done), kind=kOutput, calls=%fused_computation.13 | convolution fusion | flops 12582912 | bytes 4202496 | tf_op jit(solution)/shard_map/dot_general | solution.py:62
  133.8 19.0 %all_to_all.50 = f32[64,1,1024]{2,1,0:T(1,128)S(1)} all-to-all(f32[64,1,1024]{2,1,0:T(1,128)S(1)} %broadcast_in_dim.29), channel_id=1, replica_groups=mesh['batch'=4,'proto'=64] {'proto'}, dimensions={0} | all-to-all | bytes 524288 | tf_op jit(solution)/shard_map/all_to_all | solution.py:13
  152.9 5.6 %fusion.6 = f32[1,1024]{1,0:T(1,128)S(1)} fusion(f32[1024,1]{0,1:T(1,128)S(1)} %bitcast.60, f32[1024,1024]{1,0:T(8,128)} %copy-done), kind=kOutput, calls=%fused_computation.11 | convolution fusion | flops 12582912 | bytes 4202496 | tf_op jit(solution)/shard_map/dot_general | solution.py:59
  158.6 6.7 %all_to_all.51 = f32[4,1,1024]{2,1,0:T(1,128)S(1)} all-to-all(f32[4,1,1024]{2,1,0:T(1,128)S(1)} %broadcast_in_dim.30), channel_id=1, replica_groups=mesh['batch'=4,'proto'=64] {'batch'}, dimensions={0} | all-to-all | bytes 32768 | tf_op jit(solution)/shard_map/all_to_all | solution.py:13
  165.3 4.4 %fusion.4 = f32[1,1024]{1,0:T(1,128)S(1)} fusion(f32[1024,1]{0,1:T(1,128)S(1)} %bitcast.56, f32[1024,1024]{1,0:T(8,128)} %copy-done), kind=kOutput, calls=%fused_computation.8 | convolution fusion | flops 12582912 | bytes 4202496 | tf_op jit(solution)/shard_map/dot_general | solution.py:62
  170.6 7.4 %all-to-all-start.6 = ((f32[64,1,1024]{2,1,0:T(1,128)}), f32[64,1,1024]{2,1,0:T(1,128)S(1)}, u32[]{:S(2)}, u32[]{:S(2)}) async-start(f32[64,1,1024]{2,1,0:T(1,128)} %broadcast_in_dim.31), calls=%async_computation.6 | async-start | bytes 524288 | tf_op jit(solution)/shard_map/all_to_all | solution.py:13
  178.0 2.1 multiply_reduce_fusion
  180.1 9.9 %all-to-all-done.6 = f32[64,1,1024]{2,1,0:T(1,128)S(1)} async-done(((f32[64,1,1024]{2,1,0:T(1,128)}), f32[64,1,1024]{2,1,0:T(1,128)S(1)}, u32[]{:S(2)}, u32[]{:S(2)}) %all-to-all-start.6) | async-done | bytes 262176 | tf_op jit(solution)/shard_map/all_to_all | solution.py:13
  190.2 6.9 %fusion.2 = (f32[1024]{0:T(1024)S(1)}, f32[1024]{0:T(1024)S(1)}, bf16[1024,1024]{0,1:T(8,128)(2,1)}) fusion(f32[1024]{0:T(1024)S(1)} %add_rsqrt_fusion, f32[1024]{0:T(1024)S(1)} %divide_multiply_fusion, f32[1024]{0:T(1024)S(1)} %multiply_divide_fusion, f32[1024,1024]{1,0:T(8,128)} %copy-done, bf16[1024,1024]{0,1:T(8,128)(2,1)} %all-gather.2.cloned.1.call-done, ...), kind=kOutput, calls=%fused_computation.6 | convolution fusion | flops 2160064512 | bytes 10510336 | tf_op jit(solution)/shard_map/dot_general | solution.py:37
  198.2 6.0 %all-to-all-start.7 = ((f32[64,1,2048]{2,1,0:T(1,128)}), f32[64,1,2048]{2,1,0:T(1,128)S(1)}, u32[]{:S(2)}, u32[]{:S(2)}) async-start(f32[64,1,2048]{2,1,0:T(1,128)} %broadcast_in_dim.32), calls=%async_computation.7 | async-start | bytes 1048576 | tf_op jit(solution)/shard_map/all_to_all | solution.py:13
  204.2 3.9 %copy.16 = bf16[1024,1024]{1,0:T(8,128)(2,1)} copy(bf16[1024,1024]{0,1:T(8,128)(2,1)} %get-tuple-element.12) | data formatting | bytes 4194304
  208.2 13.3 %all-to-all-done.7 = f32[64,1,2048]{2,1,0:T(1,128)S(1)} async-done(((f32[64,1,2048]{2,1,0:T(1,128)}), f32[64,1,2048]{2,1,0:T(1,128)S(1)}, u32[]{:S(2)}, u32[]{:S(2)}) %all-to-all-start.7) | async-done | bytes 524320 | tf_op jit(solution)/shard_map/all_to_all | solution.py:13
  (32 shorter events, 5.1 us)
Async XLA Ops:
  9.5 65.5 %all-to-all-start = ((bf16[64,1024,16]{1,2,0:T(8,128)(2,1)}), bf16[64,1024,16]{1,2,0:T(8,128)(2,1)S(1)}, u32[]{:S(2)}, u32[]{:S(2)}) async-start(bf16[64,1024,16]{1,2,0:T(8,128)(2,1)} %stack.2), calls=%async_computation | async-start | bytes 4194304 | tf_op jit(solution)/shard_map/all_to_all | solution.py:47
  22.7 155.4 %all-gather.2.cloned.1.call-start = ((), (), s32[]{:S(2)}) async-start(), calls=%async_computation.8 | async-start | bytes 2129920 | tf_op jit(solution)/shard_map/all_gather | solution.py:49
  79.5 1.9 copy-start
  158.6 31.6 %copy-start.1 = (bf16[1024,1024]{1,0:T(8,128)(2,1)S(1)}, bf16[1024,1024]{1,0:T(8,128)(2,1)}, u32[]{:S(2)}) copy-start(bf16[1024,1024]{1,0:T(8,128)(2,1)} %param.5) | copy-start | bytes 6291460
  170.6 19.4 %all-to-all-start.6 = ((f32[64,1,1024]{2,1,0:T(1,128)}), f32[64,1,1024]{2,1,0:T(1,128)S(1)}, u32[]{:S(2)}, u32[]{:S(2)}) async-start(f32[64,1,1024]{2,1,0:T(1,128)} %broadcast_in_dim.31), calls=%async_computation.6 | async-start | bytes 524288 | tf_op jit(solution)/shard_map/all_to_all | solution.py:13
  198.2 23.3 %all-to-all-start.7 = ((f32[64,1,2048]{2,1,0:T(1,128)}), f32[64,1,2048]{2,1,0:T(1,128)S(1)}, u32[]{:S(2)}, u32[]{:S(2)}) async-start(f32[64,1,2048]{2,1,0:T(1,128)} %broadcast_in_dim.32), calls=%async_computation.7 | async-start | bytes 1048576 | tf_op jit(solution)/shard_map/all_to_all | solution.py:13
Sparse Core Ops, SparseCore 0:
  26.2 81.1 all-gather.1
